TPU v7x, 32 devices: a whole 2x2x4 slice. The times are simulated.
32 devices in a mesh: fft: 16 (over z, x, core), band: 2 (over y).
Axes of the slice: x: 2, y: 2, z: 4, core: 2. Of those that a mesh axis runs over, the one named last changes fastest.
Arguments:
- wavefunctions: float32 [2, 4, 128, 128, 128], P(None, 'band', 'fft'), may hold values from -6 to 6
- potential: float32 [128, 128, 128], P('fft'), may hold values from -30 to 10
- occupation: float32 [4], P('band'), may hold values from 0.05 to 1
Outputs:
- propagated: float32 [2, 4, 128, 128, 128], P(None, 'band', 'fft')
- reduced_gradient: float32 [128, 128, 128], P('fft', 'band')
- exchange_density: float32 [128, 128, 128], P('fft', 'band')
All inputs are finite; a program needn't handle non-finite values.
Results may differ from a plain program's by a relative error of at most 0.0003.
Values sent between devices are 32-bit elements; how exact they have to be, the bound alone decides.
A program may use at most 64 MiB of HBM per device.

v0:
```python
import math

import jax
import jax.numpy as jnp
import numpy as np
from jax import lax
from jax.sharding import PartitionSpec as P

SPACING = 0.4
TIME_STEP = 0.012
KAPPA_PBE = 0.804
MU_PBE = 0.21951
FERMI_FACTOR = 2.0 * math.pow(3.0 * math.pi * math.pi, 1.0 / 3.0)
SLATER_FACTOR = 0.75 * math.pow(3.0 / math.pi, 1.0 / 3.0)


def second_derivative_tables(length):
    counter = np.arange(length)
    signed = np.where(counter < length // 2, counter, counter - length)
    squared = 0.5 * (signed * (2.0 * math.pi / (length * SPACING))) ** 2
    phase = (counter[:, None] * counter[None, :]) % length
    wave = np.cos(phase * (2.0 * math.pi / length))
    once = wave @ squared / length
    twice = wave @ (squared * squared) / length
    offset = (counter[:, None] - counter[None, :]) % length
    return (once[offset].astype(np.float32), twice[offset].astype(np.float32))


def along(values, table, formula):
    return jnp.einsum(
        formula,
        values,
        table,
        precision=lax.Precision.HIGHEST,
        preferred_element_type=jnp.float32,
    )


def in_plane(values, table):
    return along(values, table, "kzxy,xe->kzey") + along(values, table, "kzxy,ye->kzxe")


def to_columns(values):
    return lax.all_to_all(values, "fft", split_axis=2, concat_axis=1, tiled=True)


def to_planes(values):
    return lax.all_to_all(values, "fft", split_axis=1, concat_axis=2, tiled=True)


def fourth_order(padded, dimension):
    length = padded.shape[dimension] - 4

    def shifted(offset):
        return lax.slice_in_dim(padded, offset, offset + length, axis=dimension)

    return (8.0 * (shifted(3) - shifted(1)) - (shifted(4) - shifted(0))) / (12.0 * SPACING)


def periodic_derivative(values, dimension):
    nearer = jnp.roll(values, -1, dimension) - jnp.roll(values, 1, dimension)
    farther = jnp.roll(values, -2, dimension) - jnp.roll(values, 2, dimension)
    return (8.0 * nearer - farther) / (12.0 * SPACING)


def exchange_terms(density, grad_z, grad_x, grad_y):
    gradient_norm = jnp.sqrt(grad_z * grad_z + grad_x * grad_x + grad_y * grad_y)
    power = jnp.power(density, 4.0 / 3.0)
    reduced = gradient_norm / (FERMI_FACTOR * power)
    enhance = 1.0 + KAPPA_PBE - KAPPA_PBE / (1.0 + MU_PBE * reduced * reduced / KAPPA_PBE)
    return (reduced, -SLATER_FACTOR * power * enhance)


def padded_density(partial):
    slabs, groups = (lax.axis_size("fft"), lax.axis_size("band"))
    width = partial.shape[1] // groups
    extended = jnp.concatenate([partial[:, -2:], partial, partial[:, :2]], axis=1)
    own = lax.axis_index("band")
    center, before, after = (0.0, 0.0, 0.0)
    for step in range(groups):
        target = lax.rem(own + step, groups)
        window = lax.dynamic_slice_in_dim(extended, target * width, width + 4, axis=1)

        def send(values, shift):
            pairs = [
                (f * groups + b, (f + shift) % slabs * groups + (b + step) % groups)
                for f in range(slabs)
                for b in range(groups)
            ]
            return lax.ppermute(values, ("fft", "band"), pairs)

        before = before + send(window[-2:], 1)
        after = after + send(window[:2], -1)
        center = center + (window if step == 0 else send(window, 0))
    return jnp.concatenate([before, center, after], axis=0)


def per_device(wavefunctions, potential, occupation):
    parts, bands, depth, length, _ = wavefunctions.shape
    once, twice = second_derivative_tables(length)
    field = wavefunctions.reshape(parts * bands, depth, length, length)
    columns = to_columns(jnp.concatenate([field, potential[None]], axis=0))
    local = in_plane(field, once) + potential * field
    field_columns, potential_columns = (columns[:-1], columns[-1:])
    normal_columns = along(field_columns, once, "kzxy,ze->kexy")
    normal = to_planes(normal_columns)
    weighted_columns = normal_columns + potential_columns * field_columns
    normal_second = to_planes(along(weighted_columns, once, "kzxy,ze->kexy"))
    first = normal + local
    second = in_plane(normal + first, once) + potential * first + normal_second
    shape = wavefunctions.shape
    first = first.reshape(shape)
    second = second.reshape(shape)
    result = jnp.stack([
        wavefunctions[0] + TIME_STEP * first[1] - 0.5 * TIME_STEP * TIME_STEP * second[0],
        wavefunctions[1] - TIME_STEP * first[0] - 0.5 * TIME_STEP * TIME_STEP * second[1],
    ])
    squares = result[0] * result[0] + result[1] * result[1]
    padded = padded_density(jnp.sum(occupation[:, None, None, None] * squares, axis=0))
    center = padded[2:-2, 2:-2]
    grad_z = fourth_order(padded[:, 2:-2], 0)
    grad_x = fourth_order(padded[2:-2], 1)
    grad_y = periodic_derivative(center, 2)
    reduced, energy = exchange_terms(center, grad_z, grad_x, grad_y)
    return (result, reduced, energy)


def solution(mesh):
    in_specs = (P(None, "band", "fft", None, None), P("fft", None, None), P("band"))
    out_specs = (P(None, "band", "fft", None, None), P("fft", "band", None), P("fft", "band", None))
    return jax.shard_map(
        per_device, mesh=mesh, in_specs=in_specs, out_specs=out_specs, check_vma=False
    )
```

profile of v0, /device:TPU:0, one launch (start us, length us, event | category | flops | bytes accessed | tf_op | source)
XLA Modules:
  0.0 210.1 jit_solution(11403077479704691160)
XLA Ops:
  0.6 1.9 pad_maximum_fusion
  2.6 1.5 copy.48
  4.1 65.6 %all_to_all.51 = f32[5,8,128,128]{3,1,0,2:T(8,128)S(1)} all-to-all(f32[5,8,128,128]{3,1,0,2:T(8,128)S(1)} %copy.48), channel_id=1, replica_groups=mesh['fft'=16,'band'=2] {'fft'}, dimensions={2} | all-to-all | bytes 5242880 | tf_op jit(solution)/shard_map/all_to_all | solution.py:44
  69.7 0.5 copy.82
  70.2 0.0 copy-start.3
  70.2 0.2 slice.158
  70.4 1.3 copy-done.3
  71.7 1.6 copy.50
  73.3 2.0 copy.51
  75.2 0.0 copy-done.5
  75.2 3.1 %convolution_bitcast_fusion = f32[4,128,8,128]{1,3,2,0:T(8,128)} fusion(f32[4,128,8,128]{1,3,2,0:T(8,128)S(1)} %copy.51, f32[128,128,1,1]{1,0,3,2:T(8,128)S(1)} %copy-done.5), kind=kOutput, calls=%fused_computation.14 | convolution fusion | flops 805306368 | bytes 4259840 | tf_op jit(solution)/shard_map/kzxy,ze->kexy/dot_general | solution.py:30
  78.4 3.1 %copy.52 = f32[4,128,8,128]{3,2,0,1:T(8,128)} copy(f32[4,128,8,128]{1,3,2,0:T(8,128)} %convolution_bitcast_fusion) | data formatting | bytes 4194304 | tf_op jit(solution)/shard_map/kzxy,ze->kexy/transpose | solution.py:30
  81.4 5.2 %all-to-all-start.1 = ((f32[4,128,8,128]{3,2,0,1:T(8,128)}), f32[4,128,8,128]{3,2,0,1:T(8,128)}, u32[]{:S(2)}, u32[]{:S(2)}) async-start(f32[4,128,8,128]{3,2,0,1:T(8,128)} %copy.52), calls=%async_computation.1 | async-start | bytes 4194304 | tf_op jit(solution)/shard_map/all_to_all | solution.py:48
  86.6 1.1 slice.160
  87.8 0.2 copy.61
  88.0 4.8 %fusion.6 = f32[4,128,8,128]{1,3,2,0:T(8,128)} fusion(f32[128,128,1,1]{1,0,3,2:T(8,128)S(1)} %copy-done.5, f32[4,128,8,128]{1,3,2,0:T(8,128)} %convolution_bitcast_fusion, f32[4,128,8,128]{1,3,2,0:T(8,128)S(1)} %copy.51, f32[128,8,128]{0,2,1:T(8,128)S(1)} %copy.61), kind=kOutput, calls=%fused_computation.13 | convolution fusion | flops 806354944 | bytes 6881280 | tf_op jit(solution)/shard_map/kzxy,ze->kexy/dot_general | solution.py:30
  92.8 3.2 %copy.63 = f32[4,128,8,128]{3,2,0,1:T(8,128)} copy(f32[4,128,8,128]{1,3,2,0:T(8,128)} %fusion.6) | data formatting | bytes 4194304 | tf_op jit(solution)/shard_map/kzxy,ze->kexy/transpose | solution.py:30
  95.9 31.7 %all-to-all-done.1 = f32[4,128,8,128]{3,2,0,1:T(8,128)} async-done(((f32[4,128,8,128]{3,2,0,1:T(8,128)}), f32[4,128,8,128]{3,2,0,1:T(8,128)}, u32[]{:S(2)}, u32[]{:S(2)}) %all-to-all-start.1) | async-done | bytes 2097184 | tf_op jit(solution)/shard_map/all_to_all | solution.py:48
  127.7 11.3 %all-to-all-start.2 = ((f32[4,128,8,128]{3,2,0,1:T(8,128)}), f32[4,128,8,128]{3,2,0,1:T(8,128)}, u32[]{:S(2)}, u32[]{:S(2)}) async-start(f32[4,128,8,128]{3,2,0,1:T(8,128)} %copy.63), calls=%async_computation.2 | async-start | bytes 4194304 | tf_op jit(solution)/shard_map/all_to_all | solution.py:48
  139.0 0.0 copy-done
  139.0 0.0 copy-start.4
  139.0 1.9 fusion.49
  140.9 0.0 copy-done.4
  140.9 3.8 %fusion.2 = f32[4,8,128,128]{3,2,1,0:T(8,128)S(1)} fusion(f32[128,4,8,128]{3,0,2,1:T(8,128)S(1)} %fusion.49, f32[4,8,128,128]{3,2,1,0:T(8,128)S(1)} %bitcast.88, f32[4,8,16,8,128]{4,3,0,1,2:T(8,128)} %bitcast.10, f32[128,128,1,1]{1,0,3,2:T(8,128)S(1)} %copy-done.5, f32[8,128,128]{2,1,0:T(8,128)S(1)} %copy-done.4), kind=kOutput, calls=%fused_computation.8 | convolution fusion | flops 807403520 | bytes 8978432 | tf_op jit(solution)/shard_map/kzxy,ye->kzxe/dot_general | solution.py:30
  144.7 0.0 copy-start.1
  144.7 1.3 copy-done.1
  146.1 4.8 %fusion.17 = f32[4,8,128,128]{3,2,1,0:T(8,128)} fusion(f32[128,128,1,1]{1,0,3,2:T(8,128)S(1)} %copy-done.5, f32[4,8,128,128]{3,2,1,0:T(8,128)S(1)} %fusion.2, f32[4,8,16,8,128]{4,3,0,1,2:T(8,128)} %bitcast.10), kind=kOutput, calls=%fused_computation.33 | convolution fusion | flops 805830656 | bytes 6356992 | tf_op jit(solution)/shard_map/kzxy,ye->kzxe/dot_general | solution.py:30
  150.8 29.2 %all-to-all-done.2 = f32[4,128,8,128]{3,2,0,1:T(8,128)} async-done(((f32[4,128,8,128]{3,2,0,1:T(8,128)}), f32[4,128,8,128]{3,2,0,1:T(8,128)}, u32[]{:S(2)}, u32[]{:S(2)}) %all-to-all-start.2) | async-done | bytes 2097184 | tf_op jit(solution)/shard_map/all_to_all | solution.py:48
  180.0 6.7 %bitcast_add_fusion = f32[4,8,128,128]{3,2,1,0:T(8,128)S(1)} fusion(f32[4,8,16,8,128]{4,3,0,1,2:T(8,128)} %bitcast.24, f32[4,8,128,128]{3,2,1,0:T(8,128)} %fusion.17, f32[4,8,128,128]{3,2,1,0:T(8,128)} %copy-done.1, f32[128,128,1,1]{1,0,3,2:T(8,128)S(1)} %copy-done.5, f32[8,128,128]{2,1,0:T(8,128)S(1)} %copy-done.4, f32[4,8,16,8,128]{4,3,0,1,2:T(8,128)} %bitcast.10), kind=kOutput, calls=%fused_computation.3 | convolution fusion | flops 807927808 | bytes 11075584 | tf_op jit(solution)/shard_map/kzxy,xe->kzey/dot_general | solution.py:30
  186.7 0.0 copy-start.6
  186.7 0.8 bitcast_subtract_fusion.3
  187.5 0.8 fusion.13
  188.4 1.6 collective-permute-start
  190.0 9.5 %collective-permute-start.2 = (f32[2,68,128]{2,1,0:T(8,128)S(1)}, f32[2,68,128]{2,1,0:T(8,128)S(1)}, u32[]{:S(2)}, u32[]{:S(2)}) collective-permute-start(f32[2,68,128]{2,1,0:T(8,128)S(1)} %get-tuple-element.7), channel_id=1, source_target_pairs={{0,31},{1,30},{2,1},{3,0},{4,3},{5,2},{6,5},{7,4},{8,7},{9,6},{10,... | collective-permute-start | bytes 208904 | tf_op jit(solution)/shard_map/ppermute | solution.py:90
  199.6 0.0 collective-permute-start.4
  199.6 0.0 collective-permute-start.3
  199.6 5.4 %collective-permute-start.1 = (f32[2,68,128]{2,1,0:T(8,128)S(1)}, f32[2,68,128]{2,1,0:T(8,128)S(1)}, u32[]{:S(2)}, u32[]{:S(2)}) collective-permute-start(f32[2,68,128]{2,1,0:T(8,128)S(1)} %get-tuple-element.10), channel_id=1, source_target_pairs={{0,30},{1,31},{2,0},{3,1},{4,2},{5,3},{6,4},{7,5},{8,6},{9,7},{10,... | collective-permute-start | bytes 208904 | tf_op jit(solution)/shard_map/ppermute | solution.py:90
  205.0 1.5 pad_maximum_fusion.1
  206.4 0.5 collective-permute-done.4
  206.9 0.8 collective-permute-done.3
  207.8 0.0 collective-permute-done.2
  207.8 0.0 collective-permute-done.1
  207.8 0.0 collective-permute-done
  207.9 0.1 fusion.47
  208.0 0.1 fusion.46
  208.2 0.1 fusion.45
  208.3 0.1 fusion.48
  208.5 1.6 fusion.33
  (13 shorter events, 0.2 us)
Async XLA Ops:
  70.2 1.5 copy-start.3
  73.3 2.0 copy-start.5
  81.4 46.3 %all-to-all-start.1 = ((f32[4,128,8,128]{3,2,0,1:T(8,128)}), f32[4,128,8,128]{3,2,0,1:T(8,128)}, u32[]{:S(2)}, u32[]{:S(2)}) async-start(f32[4,128,8,128]{3,2,0,1:T(8,128)} %copy.52), calls=%async_computation.1 | async-start | bytes 4194304 | tf_op jit(solution)/shard_map/all_to_all | solution.py:48
  95.9 43.1 %copy-start = (f32[2,2,8,128,128]{4,3,2,1,0:T(8,128)S(1)}, f32[2,2,8,128,128]{4,3,2,1,0:T(8,128)}, u32[]{:S(2)}) copy-start(f32[2,2,8,128,128]{4,3,2,1,0:T(8,128)} %param.9) | copy-start | bytes 6291460
  127.7 52.3 %all-to-all-start.2 = ((f32[4,128,8,128]{3,2,0,1:T(8,128)}), f32[4,128,8,128]{3,2,0,1:T(8,128)}, u32[]{:S(2)}, u32[]{:S(2)}) async-start(f32[4,128,8,128]{3,2,0,1:T(8,128)} %copy.63), calls=%async_computation.2 | async-start | bytes 4194304 | tf_op jit(solution)/shard_map/all_to_all | solution.py:48
  139.0 1.9 copy-start.4
  144.7 1.3 copy-start.1
  180.0 6.7 %copy-start.2 = (f32[4,8,128,128]{3,2,1,0:T(8,128)S(1)}, f32[4,8,128,128]{3,2,1,0:T(8,128)}, u32[]{:S(2)}) copy-start(f32[4,8,128,128]{3,2,1,0:T(8,128)} %copy-done.1) | copy-start | bytes 6291460
  186.7 0.8 copy-start.6
  188.4 19.4 %collective-permute-start = (f32[8,68,128]{2,1,0:T(8,128)S(1)}, f32[8,68,128]{2,1,0:T(8,128)S(1)}, u32[]{:S(2)}, u32[]{:S(2)}) collective-permute-start(f32[8,68,128]{2,1,0:T(8,128)S(1)} %constant_dynamic-slice_fusion.4), channel_id=1, source_target_pairs={{0,1},{1,0},{2,3},{3,2},{4,5},{5,4},{6,7},{7,6},{8,9},{9,8},{10,11... | collective-permute-start | bytes 835592 | tf_op jit(solution)/shard_map/ppermute | solution.py:90
  190.0 17.8 %collective-permute-start.2 = (f32[2,68,128]{2,1,0:T(8,128)S(1)}, f32[2,68,128]{2,1,0:T(8,128)S(1)}, u32[]{:S(2)}, u32[]{:S(2)}) collective-permute-start(f32[2,68,128]{2,1,0:T(8,128)S(1)} %get-tuple-element.7), channel_id=1, source_target_pairs={{0,31},{1,30},{2,1},{3,0},{4,3},{5,2},{6,5},{7,4},{8,7},{9,6},{10,... | collective-permute-start | bytes 208904 | tf_op jit(solution)/shard_map/ppermute | solution.py:90
  199.6 7.4 %collective-permute-start.4 = (f32[2,68,128]{2,1,0:T(8,128)S(1)}, f32[2,68,128]{2,1,0:T(8,128)S(1)}, u32[]{:S(2)}, u32[]{:S(2)}) collective-permute-start(f32[2,68,128]{2,1,0:T(8,128)S(1)} %get-tuple-element.8), channel_id=1, source_target_pairs={{0,3},{1,2},{2,5},{3,4},{4,7},{5,6},{6,9},{7,8},{8,11},{9,10},{10,... | collective-permute-start | bytes 208904 | tf_op jit(solution)/shard_map/ppermute | solution.py:90
  199.6 8.2 %collective-permute-start.3 = (f32[2,68,128]{2,1,0:T(8,128)S(1)}, f32[2,68,128]{2,1,0:T(8,128)S(1)}, u32[]{:S(2)}, u32[]{:S(2)}) collective-permute-start(f32[2,68,128]{2,1,0:T(8,128)S(1)} %get-tuple-element.9), channel_id=1, source_target_pairs={{0,2},{1,3},{2,4},{3,5},{4,6},{5,7},{6,8},{7,9},{8,10},{9,11},{10,... | collective-permute-start | bytes 208904 | tf_op jit(solution)/shard_map/ppermute | solution.py:90
  199.6 8.2 %collective-permute-start.1 = (f32[2,68,128]{2,1,0:T(8,128)S(1)}, f32[2,68,128]{2,1,0:T(8,128)S(1)}, u32[]{:S(2)}, u32[]{:S(2)}) collective-permute-start(f32[2,68,128]{2,1,0:T(8,128)S(1)} %get-tuple-element.10), channel_id=1, source_target_pairs={{0,30},{1,31},{2,0},{3,1},{4,2},{5,3},{6,4},{7,5},{8,6},{9,7},{10,... | collective-permute-start | bytes 208904 | tf_op jit(solution)/shard_map/ppermute | solution.py:90
where the time goes:
time: 211 us; the launch traced here: 210 us
  blocking collectives  65.6 us (31%)
  waiting for transfers between devices  62.3 us (30%)
  starting transfers between devices  33 us (16%)
  matrix products  25 us (12%)
  local copies, waits for them, and re-layouts  16.6 us (8%)
  other arithmetic  6.7 us (3%)
    all_to_all x1, blocking collectives, to_columns(): lax.all_to_all(values, 'fft', split_axis=2, concat_axis=1, tiled=True)  65.6 us
    all_to_all x2, waiting for transfers between devices, to_planes(): lax.all_to_all(values, 'fft', split_axis=1, concat_axis=2, tiled=True)  60.9 us
    dot_general x6, matrix products, along(): jnp.einsum(formula, values, table, precision=lax.Precision.HIGHEST, prefe...  25 us
    ppermute x5, starting transfers between devices, send(): return lax.ppermute(values, ('fft', 'band'), pairs)  16.5 us
    all_to_all x2, starting transfers between devices, to_planes(): lax.all_to_all(values, 'fft', split_axis=1, concat_axis=2, tiled=True)  16.5 us
    transpose x2, local copies, waits for them, and re-layouts, along(): jnp.einsum(formula, values, table, precision=lax.Precision.HIGHEST, prefe...  6.21 us
    slice x5, local copies, waits for them, and re-layouts, per_device(): field_columns, potential_columns = (columns[:-1], columns[-1:])  4.89 us
  transfers between devices with their start and end apart: 7, of which 4 were waited for; matrix products, arithmetic and copies ran while one was open for 10% of the time, Pallas kernels for 0%

commit v1 on v0

--- a/solution.py
+++ b/solution.py
@@ -1,9 +1,12 @@
+import functools
 import math
 
 import jax
 import jax.numpy as jnp
 import numpy as np
 from jax import lax
+from jax.experimental import pallas as pl
+from jax.experimental.pallas import tpu as pltpu
 from jax.sharding import PartitionSpec as P
 
 SPACING = 0.4
@@ -14,16 +17,14 @@
 SLATER_FACTOR = 0.75 * math.pow(3.0 / math.pi, 1.0 / 3.0)
 
 
-def second_derivative_tables(length):
+def second_derivative(length):
     counter = np.arange(length)
     signed = np.where(counter < length // 2, counter, counter - length)
     squared = 0.5 * (signed * (2.0 * math.pi / (length * SPACING))) ** 2
     phase = (counter[:, None] * counter[None, :]) % length
     wave = np.cos(phase * (2.0 * math.pi / length))
-    once = wave @ squared / length
-    twice = wave @ (squared * squared) / length
     offset = (counter[:, None] - counter[None, :]) % length
-    return (once[offset].astype(np.float32), twice[offset].astype(np.float32))
+    return (wave @ squared / length)[offset].astype(np.float32)
 
 
 def along(values, table, formula):
@@ -95,9 +96,9 @@
     return jnp.concatenate([before, center, after], axis=0)
 
 
-def per_device(wavefunctions, potential, occupation):
+def step_with_collectives(wavefunctions, potential, occupation):
     parts, bands, depth, length, _ = wavefunctions.shape
-    once, twice = second_derivative_tables(length)
+    once = second_derivative(length)
     field = wavefunctions.reshape(parts * bands, depth, length, length)
     columns = to_columns(jnp.concatenate([field, potential[None]], axis=0))
     local = in_plane(field, once) + potential * field
@@ -116,7 +117,314 @@
         wavefunctions[1] - TIME_STEP * first[0] - 0.5 * TIME_STEP * TIME_STEP * second[1],
     ])
     squares = result[0] * result[0] + result[1] * result[1]
-    padded = padded_density(jnp.sum(occupation[:, None, None, None] * squares, axis=0))
+    partial = jnp.sum(occupation[:, None, None, None] * squares, axis=0)
+    return (result, padded_density(partial))
+
+
+MESH = pl.DeviceIdType.MESH
+EDGE = 8
+
+
+def multiply(left, right):
+    return jnp.dot(
+        left,
+        right,
+        precision=lax.Precision.HIGHEST,
+        preferred_element_type=jnp.float32,
+    )
+
+
+def step_kernel(
+    slabs, groups, psi, pot, occ, table, out, dens,
+    psi_v, pot_v, psi_col, pot_col, normal_col, second_col, normal, second, local,
+    result, partial, arrived,
+    send_sem, recv_sem, local_sem, dens_send, dens_recv,
+):
+    parts, bands, depth, length, _ = psi.shape
+    rows = length // slabs
+    width = length // groups
+    me = lax.axis_index("fft")
+    own = lax.axis_index("band")
+    half = 0.5 * TIME_STEP * TIME_STEP
+
+    barrier = pltpu.get_barrier_semaphore()
+
+    def greet(step, carry):
+        peer = lax.rem(me + step, slabs)
+        pl.semaphore_signal(barrier, inc=1, device_id={"fft": peer}, device_id_type=MESH)
+        return carry
+
+    lax.fori_loop(1, slabs, greet, 0)
+    count = slabs - 1
+    for group in range(1, groups):
+        for shift in (0, 1, slabs - 1):
+            there = {"fft": lax.rem(me + shift, slabs), "band": lax.rem(own + group, groups)}
+            pl.semaphore_signal(barrier, inc=1, device_id=there, device_id_type=MESH)
+            count += 1
+
+    load_psi = pltpu.make_async_copy(psi, psi_v, local_sem.at[0])
+    load_pot = pltpu.make_async_copy(pot, pot_v, local_sem.at[1])
+    load_psi.start()
+    load_pot.start()
+    pl.semaphore_wait(barrier, count)
+
+    def x_rows(device):
+        return pl.ds(pl.multiple_of(device * rows, rows), rows)
+
+    def z_planes(device):
+        return pl.ds(pl.multiple_of(device * depth, depth), depth)
+
+    def ends(chunk, device):
+        if chunk < bands:
+            return (psi.at[:, chunk, :, x_rows(device)], psi_col.at[chunk, :, z_planes(me)])
+        if chunk == bands:
+            return (pot.at[:, x_rows(device)], pot_col.at[z_planes(me)])
+        if chunk <= 2 * bands:
+            band = chunk - bands - 1
+            return (normal_col.at[band, :, z_planes(device)], normal.at[band, :, :, x_rows(me)])
+        band = chunk - 2 * bands - 1
+        return (second_col.at[band, :, z_planes(device)], second.at[band, :, :, x_rows(me)])
+
+    def remote(chunk, device, slot):
+        source, target = ends(chunk, device)
+        return pltpu.make_async_remote_copy(
+            src_ref=source,
+            dst_ref=target,
+            send_sem=send_sem.at[chunk, device],
+            recv_sem=recv_sem.at[chunk, slot],
+            device_id={"fft": device},
+            device_id_type=MESH,
+        )
+
+    def keep(chunk):
+        source, target = ends(chunk, me)
+        return pltpu.make_async_copy(source, target, local_sem.at[2 + chunk])
+
+    def post(chunk):
+        def one(step, carry):
+            remote(chunk, lax.rem(me + step, slabs), me).start()
+            return carry
+
+        lax.fori_loop(1, slabs, one, 0)
+        keep(chunk).start()
+
+    def collect(chunk):
+        def one(step, carry):
+            device = lax.rem(me + slabs - step, slabs)
+            remote(chunk, device, device).wait_recv()
+            return carry
+
+        lax.fori_loop(1, slabs, one, 0)
+        keep(chunk).wait()
+
+    for chunk in range(bands + 1):
+        post(chunk)
+
+    matrix = table[...]
+    load_psi.wait()
+    load_pot.wait()
+
+    def in_planes(index, carry):
+        part = index // (bands * depth)
+        band = index // depth % bands
+        z = index % depth
+        values = psi_v[part, band, z]
+        local[band, part, z] = (
+            multiply(matrix, values) + multiply(values, matrix) + pot_v[z] * values
+        )
+        return carry
+
+    lax.fori_loop(0, parts * bands * depth, in_planes, 0)
+
+    def strided(ref, row):
+        return (ref.reshape(length * rows, length), pl.ds(row, length, stride=rows))
+
+    def load(ref, row):
+        flat, span = strided(ref, row)
+        return flat[span, :]
+
+    def store(ref, row, values):
+        flat, span = strided(ref, row)
+        flat[span, :] = values
+
+    for band in range(bands):
+        collect(band)
+        for part in range(parts):
+            for row in range(rows):
+                values = load(psi_col.at[band, part], row)
+                store(normal_col.at[band, part], row, multiply(matrix, values))
+        post(bands + 1 + band)
+    collect(bands)
+    for band in range(bands):
+        for part in range(parts):
+            for row in range(rows):
+                values = load(normal_col.at[band, part], row)
+                values += load(pot_col, row) * load(psi_col.at[band, part], row)
+                store(second_col.at[band, part], row, multiply(matrix, values))
+        post(2 * bands + 1 + band)
+
+    for band in range(bands):
+        collect(bands + 1 + band)
+
+        def advance(z, carry):
+            firsts = []
+            seconds = []
+            for part in range(parts):
+                kinetic = normal[band, part, z]
+                first = kinetic + local[band, part, z]
+                both = kinetic + first
+                firsts.append(first)
+                seconds.append(
+                    multiply(matrix, both) + multiply(both, matrix) + pot_v[z] * first
+                )
+            result[0, band, z] = psi_v[0, band, z] + TIME_STEP * firsts[1] - half * seconds[0]
+            result[1, band, z] = psi_v[1, band, z] - TIME_STEP * firsts[0] - half * seconds[1]
+            return carry
+
+        lax.fori_loop(0, depth, advance, 0)
+
+    for band in range(bands):
+        collect(2 * bands + 1 + band)
+        weight = occ[band]
+
+        def finish(z, carry):
+            real = result[0, band, z] - half * second[band, 0, z]
+            imag = result[1, band, z] - half * second[band, 1, z]
+            result[0, band, z] = real
+            result[1, band, z] = imag
+            share = weight * (real * real + imag * imag)
+            partial[z] = share if band == 0 else partial[z] + share
+            return carry
+
+        lax.fori_loop(0, depth, finish, 0)
+
+    def window_copies(group):
+        target = lax.rem(own + group, groups)
+        spans = (
+            (lax.rem(target * width + length - EDGE, length), 0, EDGE),
+            (target * width, EDGE, width),
+            (lax.rem(target * width + width, length), EDGE + width, EDGE),
+        )
+        found = []
+        for shift, z_from, z_to, planes in (
+            (1, depth - 2, 0, 2), (slabs - 1, 0, depth + 2, 2), (0, 0, 2, depth),
+        ):
+            if shift == 0 and group == 0:
+                continue
+            there = {"fft": lax.rem(me + shift, slabs), "band": target}
+            for x_from, x_to, size in spans:
+                slot = len(found)
+                found.append(pltpu.make_async_remote_copy(
+                    src_ref=partial.at[pl.ds(z_from, planes), pl.ds(pl.multiple_of(x_from, EDGE), size)],
+                    dst_ref=arrived.at[group, pl.ds(z_to, planes), pl.ds(x_to, size)],
+                    send_sem=dens_send.at[group, slot],
+                    recv_sem=dens_recv.at[group, slot],
+                    device_id=there,
+                    device_id_type=MESH,
+                ))
+        return found
+
+    exchange = [copy for group in reversed(range(groups)) for copy in window_copies(group)]
+    for copy in exchange:
+        copy.start()
+    write = pltpu.make_async_copy(result, out, local_sem.at[0])
+    write.start()
+    keep_window = []
+    for slot, (x_from, x_to, size) in enumerate((
+        (lax.rem(own * width + length - EDGE, length), 0, EDGE),
+        (own * width, EDGE, width),
+        (lax.rem(own * width + width, length), EDGE + width, EDGE),
+    )):
+        copy = pltpu.make_async_copy(
+            partial.at[:, pl.ds(pl.multiple_of(x_from, EDGE), size)],
+            arrived.at[0, pl.ds(2, depth), pl.ds(x_to, size)],
+            dens_send.at[groups, slot],
+        )
+        copy.start()
+        keep_window.append(copy)
+
+    for chunk in range(3 * bands + 1):
+        def drain(step, carry):
+            remote(chunk, lax.rem(me + step, slabs), me).wait_send()
+            return carry
+
+        lax.fori_loop(1, slabs, drain, 0)
+    for copy in keep_window:
+        copy.wait()
+    for copy in exchange:
+        copy.wait_recv()
+
+    def total(z, carry):
+        value = arrived[0, z]
+        for group in range(1, groups):
+            value += arrived[group, z]
+        dens[z] = value
+        return carry
+
+    lax.fori_loop(0, depth + 4, total, 0)
+    for copy in exchange:
+        copy.wait_send()
+    write.wait()
+
+
+def step_in_kernel(wavefunctions, potential, occupation):
+    parts, bands, depth, length, _ = wavefunctions.shape
+    slabs, groups = (lax.axis_size("fft"), lax.axis_size("band"))
+    rows, width = (length // slabs, length // groups)
+    table = jnp.asarray(second_derivative(length))
+    chunks = 3 * bands + 1
+    by_band = pltpu.VMEM((bands, parts, depth, length, length), jnp.float32)
+    by_part = pltpu.VMEM((parts, bands, depth, length, length), jnp.float32)
+    columns = pltpu.VMEM((bands, parts, length, rows, length), jnp.float32)
+    plane = (width + 2 * EDGE, length)
+    result, padded = pl.pallas_call(
+        functools.partial(step_kernel, slabs, groups),
+        out_shape=(
+            jax.ShapeDtypeStruct(wavefunctions.shape, jnp.float32),
+            jax.ShapeDtypeStruct((depth + 4,) + plane, jnp.float32),
+        ),
+        in_specs=[
+            pl.BlockSpec(memory_space=pl.ANY),
+            pl.BlockSpec(memory_space=pl.ANY),
+            pl.BlockSpec(memory_space=pltpu.SMEM),
+            pl.BlockSpec(memory_space=pltpu.VMEM),
+        ],
+        out_specs=(
+            pl.BlockSpec(memory_space=pl.ANY),
+            pl.BlockSpec(memory_space=pltpu.VMEM),
+        ),
+        scratch_shapes=[
+            by_part,
+            pltpu.VMEM((depth, length, length), jnp.float32),
+            columns,
+            pltpu.VMEM((length, rows, length), jnp.float32),
+            columns,
+            columns,
+            by_band,
+            by_band,
+            by_band,
+            by_part,
+            pltpu.VMEM((depth, length, length), jnp.float32),
+            pltpu.VMEM((groups, depth + 4) + plane, jnp.float32),
+            pltpu.SemaphoreType.DMA((chunks, slabs)),
+            pltpu.SemaphoreType.DMA((chunks, slabs)),
+            pltpu.SemaphoreType.DMA((chunks + 2,)),
+            pltpu.SemaphoreType.DMA((groups + 1, 9)),
+            pltpu.SemaphoreType.DMA((groups, 9)),
+        ],
+        compiler_params=pltpu.CompilerParams(
+            collective_id=0, has_side_effects=True, vmem_limit_bytes=48 * 1024 * 1024
+        ),
+    )(wavefunctions, potential, occupation, table)
+    return (result, padded[:, EDGE - 2 : EDGE + width + 2])
+
+
+def per_device(wavefunctions, potential, occupation):
+    _, _, depth, length, _ = wavefunctions.shape
+    rows = length // lax.axis_size("fft")
+    whole_tiles = rows % 8 == 0 and depth % 8 == 0 and lax.axis_size("band") == 2
+    step = step_in_kernel if whole_tiles else step_with_collectives
+    result, padded = step(wavefunctions, potential, occupation)
     center = padded[2:-2, 2:-2]
     grad_z = fourth_order(padded[:, 2:-2], 0)
     grad_x = fourth_order(padded[2:-2], 1)

time: 211 us -> 176 us (0.83)
  Pallas kernels: 0 us -> 165 us
  blocking collectives: 65.6 us -> 0 us
  waiting for transfers between devices: 62.3 us -> 0 us
  starting transfers between devices: 33 us -> 0 us
  matrix products: 25 us -> 0 us
  local copies, waits for them, and re-layouts: 16.6 us -> 5.97 us
  other arithmetic: 6.7 us -> 1.62 us
    pallas_call x0 -> x1, Pallas kernels: none -> 165 us  [step_in_kernel(): pl.pallas_call(functools.partial(step_kernel, slabs, groups), out_shape=(...]
    all_to_all x1 -> x0, blocking collectives: 65.6 us -> none  [to_columns(): lax.all_to_all(values, 'fft', split_axis=2, concat_axis=1, tiled=True)]
    all_to_all x2 -> x0, waiting for transfers between devices: 60.9 us -> none  [to_planes(): lax.all_to_all(values, 'fft', split_axis=1, concat_axis=2, tiled=True)]
    dot_general x6 -> x0, matrix products: 25 us -> none  [along(): jnp.einsum(formula, values, table, precision=lax.Precision.HIGHEST, prefe...]
    ppermute x5 -> x0, starting transfers between devices: 16.5 us -> none  [send(): return lax.ppermute(values, ('fft', 'band'), pairs)]
    all_to_all x2 -> x0, starting transfers between devices: 16.5 us -> none  [to_planes(): lax.all_to_all(values, 'fft', split_axis=1, concat_axis=2, tiled=True)]
    transpose x2 -> x0, local copies, waits for them, and re-layouts: 6.21 us -> none  [along(): jnp.einsum(formula, values, table, precision=lax.Precision.HIGHEST, prefe...]
    slice x7 -> x0, local copies, waits for them, and re-layouts: 4.93 us -> none  [the longest x5 4.89 us: per_device(): field_columns, potential_columns = (columns[:-1], columns[-1:])]
  transfers between devices with their start and end apart: 7 -> 0, of which waited for: 4 -> 0; matrix products, arithmetic and copies ran while one was open for 10% -> 0% of each run, Pallas kernels for 0% -> 0%
where the time goes in v1:
time: 176 us; the launch traced here: 173 us
  Pallas kernels  165 us (94%)
  local copies, waits for them, and re-layouts  5.97 us (3%)
    pallas_call x1, Pallas kernels, step_in_kernel(): pl.pallas_call(functools.partial(step_kernel, slabs, groups), out_shape=(...  165 us
    unnamed x9, local copies, waits for them, and re-layouts  5.44 us

profile of v1, /device:TPU:0, one launch (start us, length us, event | category | flops | bytes accessed | tf_op | source)
XLA Modules:
  0.0 173.1 jit_solution(2320100952741353057)
XLA Ops:
  0.6 0.0 copy-start
  0.6 1.6 copy-done
  2.2 0.0 copy-start.1
  2.2 1.0 copy-done.1
  3.3 0.0 copy-start.2
  3.3 0.8 copy-done.2
  4.1 0.0 copy-start.3
  4.1 0.7 copy-done.3
  4.8 164.9 %shard_map.67 = (f32[2,2,8,128,128]{4,3,2,1,0:T(8,128)S(1)}, f32[12,80,128]{2,1,0:T(8,128)S(1)}) custom-call(f32[2,2,8,128,128]{4,3,2,1,0:T(8,128)S(1)} %copy-done, f32[8,128,128]{2,1,0:T(8,128)S(1)} %copy-done.1, f32[2]{0:T(128)S(1)} %copy-done.3, f32[128,128]{1,0:T(8,128)S(1)} %copy-done.2), custom_call_target="tpu_custom_call" | custom-call | tf_op jit(solution)/shard_map/pallas_call | solution.py:380
  169.6 0.1 fusion.14
  169.8 0.1 fusion.16
  169.9 0.1 fusion.15
  170.0 0.1 fusion.13
  170.2 1.6 fusion.4
  171.8 1.3 copy.8
Async XLA Ops:
  0.6 1.6 copy-start
  2.2 1.0 copy-start.1
  3.3 0.8 copy-start.2
  4.1 0.7 copy-start.3

commit v2 on v1

--- a/solution.py
+++ b/solution.py
@@ -138,13 +138,18 @@
     slabs, groups, psi, pot, occ, table, out, dens,
     psi_v, pot_v, psi_col, pot_col, normal_col, second_col, normal, second, local,
     result, partial, arrived,
-    send_sem, recv_sem, local_sem, dens_send, dens_recv,
+    send_sem, recv_sem, local_sem, dens_send, dens_recv, pot_send, pot_recv,
 ):
     parts, bands, depth, length, _ = psi.shape
-    rows = length // slabs
+    fields = bands * parts
+    members = slabs // 2
+    rows = length // members
+    share_rows = rows // groups
     width = length // groups
     me = lax.axis_index("fft")
     own = lax.axis_index("band")
+    place = lax.rem(me, members)
+    base = me - place
     half = 0.5 * TIME_STEP * TIME_STEP
 
     barrier = pltpu.get_barrier_semaphore()
@@ -169,21 +174,43 @@
     pl.semaphore_wait(barrier, count)
 
     def x_rows(device):
-        return pl.ds(pl.multiple_of(device * rows, rows), rows)
+        return pl.ds(pl.multiple_of(lax.rem(device, members) * rows, rows), rows)
 
     def z_planes(device):
         return pl.ds(pl.multiple_of(device * depth, depth), depth)
 
+    def half_planes(device):
+        return pl.ds(pl.multiple_of(lax.rem(device, members) * depth, depth), depth)
+
+    def shared(start, group):
+        first = start + group * share_rows
+        return pl.ds(pl.multiple_of(first, share_rows), share_rows)
+
     def ends(chunk, device):
-        if chunk < bands:
-            return (psi.at[:, chunk, :, x_rows(device)], psi_col.at[chunk, :, z_planes(me)])
-        if chunk == bands:
-            return (pot.at[:, x_rows(device)], pot_col.at[z_planes(me)])
-        if chunk <= 2 * bands:
-            band = chunk - bands - 1
-            return (normal_col.at[band, :, z_planes(device)], normal.at[band, :, :, x_rows(me)])
-        band = chunk - 2 * bands - 1
-        return (second_col.at[band, :, z_planes(device)], second.at[band, :, :, x_rows(me)])
+        if chunk == fields:
+            start = lax.rem(device, members) * rows
+            return (pot.at[:, shared(start, own)], pot_col.at[z_planes(me), shared(0, own)])
+        kind, field = divmod(chunk - (chunk > fields), fields)
+        band, part = divmod(field, parts)
+        if kind == 0:
+            return (psi.at[part, band, :, x_rows(device)], psi_col.at[band, part, z_planes(me)])
+        if kind == 1:
+            return (
+                normal_col.at[band, part, z_planes(device)],
+                normal.at[band, part, :, x_rows(me)],
+            )
+        return (
+            second_col.at[band, part, half_planes(device)],
+            second.at[band, part, :, x_rows(me)],
+        )
+
+    def partners(chunk):
+        return slabs if chunk <= fields else members
+
+    def partner(chunk, step):
+        if chunk <= fields:
+            return lax.rem(me + step, slabs)
+        return base + lax.rem(place + step, members)
 
     def remote(chunk, device, slot):
         source, target = ends(chunk, device)
@@ -202,25 +229,27 @@
 
     def post(chunk):
         def one(step, carry):
-            remote(chunk, lax.rem(me + step, slabs), me).start()
+            remote(chunk, partner(chunk, step), me).start()
             return carry
 
-        lax.fori_loop(1, slabs, one, 0)
+        lax.fori_loop(1, partners(chunk), one, 0)
         keep(chunk).start()
 
     def collect(chunk):
         def one(step, carry):
-            device = lax.rem(me + slabs - step, slabs)
+            device = partner(chunk, partners(chunk) - step)
             remote(chunk, device, device).wait_recv()
             return carry
 
-        lax.fori_loop(1, slabs, one, 0)
+        lax.fori_loop(1, partners(chunk), one, 0)
         keep(chunk).wait()
 
-    for chunk in range(bands + 1):
-        post(chunk)
+    post(0)
+    post(fields)
+    post(1)
 
     matrix = table[...]
+    half_matrix = table[pl.ds(pl.multiple_of(base * depth, members * depth), members * depth), :]
     load_psi.wait()
     load_pot.wait()
 
@@ -236,35 +265,42 @@
 
     lax.fori_loop(0, parts * bands * depth, in_planes, 0)
 
-    def strided(ref, row):
-        return (ref.reshape(length * rows, length), pl.ds(row, length, stride=rows))
-
     def load(ref, row):
-        flat, span = strided(ref, row)
-        return flat[span, :]
-
-    def store(ref, row, values):
-        flat, span = strided(ref, row)
-        flat[span, :] = values
-
-    for band in range(bands):
-        collect(band)
+        return ref.reshape(length * rows, length)[pl.ds(row, length, stride=rows), :]
+
+    def store(ref, row, planes, values):
+        ref.reshape(planes * rows, length)[pl.ds(row, planes, stride=rows), :] = values
+
+    def once(field):
+        band, part = divmod(field, parts)
+        collect(field)
+        for row in range(rows):
+            values = load(psi_col.at[band, part], row)
+            store(normal_col.at[band, part], row, length, multiply(matrix, values))
+        post(fields + 1 + field)
+
+    def twice(field):
+        band, part = divmod(field, parts)
+        planes = members * depth
+        for row in range(rows):
+            values = load(normal_col.at[band, part], row)
+            values += load(pot_col, row) * load(psi_col.at[band, part], row)
+            store(second_col.at[band, part], row, planes, multiply(half_matrix, values))
+        post(2 * fields + 1 + field)
+
+    def pot_copy(group, source):
+        return pltpu.make_async_remote_copy(
+            src_ref=pot_col.at[:, shared(0, source)],
+            dst_ref=pot_col.at[:, shared(0, source)],
+            send_sem=pot_send.at[group],
+            recv_sem=pot_recv.at[group],
+            device_id={"band": lax.rem(own + group, groups)},
+            device_id_type=MESH,
+        )
+
+    def first_part(band):
         for part in range(parts):
-            for row in range(rows):
-                values = load(psi_col.at[band, part], row)
-                store(normal_col.at[band, part], row, multiply(matrix, values))
-        post(bands + 1 + band)
-    collect(bands)
-    for band in range(bands):
-        for part in range(parts):
-            for row in range(rows):
-                values = load(normal_col.at[band, part], row)
-                values += load(pot_col, row) * load(psi_col.at[band, part], row)
-                store(second_col.at[band, part], row, multiply(matrix, values))
-        post(2 * bands + 1 + band)
-
-    for band in range(bands):
-        collect(bands + 1 + band)
+            collect(fields + 1 + band * parts + part)
 
         def advance(z, carry):
             firsts = []
@@ -283,8 +319,9 @@
 
         lax.fori_loop(0, depth, advance, 0)
 
-    for band in range(bands):
-        collect(2 * bands + 1 + band)
+    def last_part(band):
+        for part in range(parts):
+            collect(2 * fields + 1 + band * parts + part)
         weight = occ[band]
 
         def finish(z, carry):
@@ -297,6 +334,29 @@
             return carry
 
         lax.fori_loop(0, depth, finish, 0)
+
+    once(0)
+    post(2)
+    collect(fields)
+    for group in range(1, groups):
+        pot_copy(group, own).start()
+    once(1)
+    for field in range(3, fields):
+        post(field)
+    for group in range(1, groups):
+        pot_copy(group, lax.rem(own + groups - group, groups)).wait_recv()
+    twice(0)
+    twice(1)
+    for field in range(2, fields - 1):
+        once(field)
+        twice(field)
+    first_part(0)
+    once(fields - 1)
+    twice(fields - 1)
+    last_part(0)
+    for band in range(1, bands):
+        first_part(band)
+        last_part(band)
 
     def window_copies(group):
         target = lax.rem(own + group, groups)
@@ -343,12 +403,14 @@
         copy.start()
         keep_window.append(copy)
 
-    for chunk in range(3 * bands + 1):
+    for chunk in range(3 * fields + 1):
         def drain(step, carry):
-            remote(chunk, lax.rem(me + step, slabs), me).wait_send()
+            remote(chunk, partner(chunk, step), me).wait_send()
             return carry
 
-        lax.fori_loop(1, slabs, drain, 0)
+        lax.fori_loop(1, partners(chunk), drain, 0)
+    for group in range(1, groups):
+        pot_copy(group, own).wait_send()
     for copy in keep_window:
         copy.wait()
     for copy in exchange:
@@ -370,9 +432,9 @@
 def step_in_kernel(wavefunctions, potential, occupation):
     parts, bands, depth, length, _ = wavefunctions.shape
     slabs, groups = (lax.axis_size("fft"), lax.axis_size("band"))
-    rows, width = (length // slabs, length // groups)
+    rows, width = (2 * length // slabs, length // groups)
     table = jnp.asarray(second_derivative(length))
-    chunks = 3 * bands + 1
+    chunks = 3 * bands * parts + 1
     by_band = pltpu.VMEM((bands, parts, depth, length, length), jnp.float32)
     by_part = pltpu.VMEM((parts, bands, depth, length, length), jnp.float32)
     columns = pltpu.VMEM((bands, parts, length, rows, length), jnp.float32)
@@ -399,7 +461,7 @@
             columns,
             pltpu.VMEM((length, rows, length), jnp.float32),
             columns,
-            columns,
+            pltpu.VMEM((bands, parts, length // 2, rows, length), jnp.float32),
             by_band,
             by_band,
             by_band,
@@ -411,9 +473,11 @@
             pltpu.SemaphoreType.DMA((chunks + 2,)),
             pltpu.SemaphoreType.DMA((groups + 1, 9)),
             pltpu.SemaphoreType.DMA((groups, 9)),
+            pltpu.SemaphoreType.DMA((groups,)),
+            pltpu.SemaphoreType.DMA((groups,)),
         ],
         compiler_params=pltpu.CompilerParams(
-            collective_id=0, has_side_effects=True, vmem_limit_bytes=48 * 1024 * 1024
+            collective_id=0, has_side_effects=True, vmem_limit_bytes=60 * 1024 * 1024
         ),
     )(wavefunctions, potential, occupation, table)
     return (result, padded[:, EDGE - 2 : EDGE + width + 2])
@@ -421,8 +485,9 @@
 
 def per_device(wavefunctions, potential, occupation):
     _, _, depth, length, _ = wavefunctions.shape
-    rows = length // lax.axis_size("fft")
-    whole_tiles = rows % 8 == 0 and depth % 8 == 0 and lax.axis_size("band") == 2
+    slabs, groups = (lax.axis_size("fft"), lax.axis_size("band"))
+    share_rows = 2 * length // slabs // groups
+    whole_tiles = slabs % 2 == 0 and groups == 2 and share_rows % 8 == 0
     step = step_in_kernel if whole_tiles else step_with_collectives
     result, padded = step(wavefunctions, potential, occupation)
     center = padded[2:-2, 2:-2]

time: 176 us -> 160 us (0.909); the launches traced: 173 us -> 159 us
  Pallas kernels: 165 us -> 153 us
  local copies, waits for them, and re-layouts: 5.97 us -> 3.97 us
    pallas_call x1, Pallas kernels: 165 us -> 153 us  [step_in_kernel(): pl.pallas_call(functools.partial(step_kernel, slabs, groups), out_shape=(...]
    unnamed x9 -> x5, local copies, waits for them, and re-layouts: 5.44 us -> 1.33 us
where the time goes in v2:
time: 160 us; the launch traced here: 159 us
  Pallas kernels  153 us (96%)
  local copies, waits for them, and re-layouts  3.97 us (2%)
  other arithmetic  1.62 us (1%)
    pallas_call x1, Pallas kernels, step_in_kernel(): pl.pallas_call(functools.partial(step_kernel, slabs, groups), out_shape=(...  153 us

profile of v2, /device:TPU:0, one launch (start us, length us, event | category | flops | bytes accessed | tf_op | source)
XLA Modules:
  0.0 159.1 jit_solution(937631077083407860)
XLA Ops:
  0.6 152.8 %shard_map.67 = (f32[2,2,8,128,128]{4,3,2,1,0:T(8,128)}, f32[12,80,128]{2,1,0:T(8,128)}) custom-call(f32[2,2,8,128,128]{4,3,2,1,0:T(8,128)} %psi.1, f32[8,128,128]{2,1,0:T(8,128)} %pot.1, f32[2]{0:T(128)} %occ.1, f32[128,128]{1,0:T(8,128)} %constant.25.clone.table), custom_call_target="tpu_custom_call" | custom-call | tf_op jit(solution)/shard_map/pallas_call | solution.py:442
  153.5 0.0 copy-start
  153.5 1.2 fusion.14
  154.7 1.2 fusion.16
  155.9 0.0 copy-done
  155.9 0.1 fusion.15
  156.0 0.1 fusion.13
  156.2 0.0 copy-start.1
  156.2 1.6 %fusion.4 = (f32[8,64,128]{2,1,0:T(8,128)}, f32[8,64,128]{2,1,0:T(8,128)}) fusion(f32[12,80,128]{2,1,0:T(8,128)S(1)} %copy-done, f32[8,64,126]{2,1,0:T(8,128)S(1)} %get-tuple-element.14, f32[8,64,2]{2,1,0:T(8,128)S(1)} %get-tuple-element.16, f32[8,64,2]{2,1,0:T(8,128)S(1)} %get-tuple-element.15, f32[8,64,126]{2,1,0:T(8,128)S(1)} %get-tuple-element.13, ...), kind=kLoop, calls=%fused_computation.5 | loop fusion | flops 2228224 | bytes 3932160 | tf_op jit(solution)/shard_map/mul | solution.py:72
  157.8 0.0 copy-done.1
  157.8 1.3 copy.8
Async XLA Ops:
  153.5 2.4 %copy-start = (f32[12,80,128]{2,1,0:T(8,128)S(1)}, f32[12,80,128]{2,1,0:T(8,128)}, u32[]{:S(2)}) copy-start(f32[12,80,128]{2,1,0:T(8,128)} %get-tuple-element.6) | copy-start | bytes 1474564
  156.2 1.6 %copy-start.1 = (f32[2,2,8,128,128]{4,3,2,1,0:T(8,128)S(1)}, f32[2,2,8,128,128]{4,3,2,1,0:T(8,128)}, u32[]{:S(2)}) copy-start(f32[2,2,8,128,128]{4,3,2,1,0:T(8,128)} %get-tuple-element.20) | copy-start | bytes 6291460

commit v3 on v2

--- a/solution.py
+++ b/solution.py
@@ -129,7 +129,7 @@
     return jnp.dot(
         left,
         right,
-        precision=lax.Precision.HIGHEST,
+        precision=lax.Precision.HIGH,
         preferred_element_type=jnp.float32,
     )
 

time: 160 us -> 159 us (level)
  no operation moved by 1% of the time
where the time goes in v3:
time: 159 us
  Pallas kernels  153 us (96%)
  local copies, waits for them, and re-layouts  3.97 us (2%)
  other arithmetic  1.62 us (1%)
    pallas_call x1, Pallas kernels, step_in_kernel(): pl.pallas_call(functools.partial(step_kernel, slabs, groups), out_shape=(...  153 us

profile of v3, /device:TPU:0, one launch (start us, length us, event | category | flops | bytes accessed | tf_op | source)
XLA Modules:
  0.0 159.1 jit_solution(10973940651429075760)
XLA Ops:
  0.6 152.8 %shard_map.67 = (f32[2,2,8,128,128]{4,3,2,1,0:T(8,128)}, f32[12,80,128]{2,1,0:T(8,128)}) custom-call(f32[2,2,8,128,128]{4,3,2,1,0:T(8,128)} %psi.1, f32[8,128,128]{2,1,0:T(8,128)} %pot.1, f32[2]{0:T(128)} %occ.1, f32[128,128]{1,0:T(8,128)} %constant.25.clone.table), custom_call_target="tpu_custom_call" | custom-call | tf_op jit(solution)/shard_map/pallas_call | solution.py:442
  153.5 0.0 copy-start
  153.5 1.2 fusion.14
  154.7 1.2 fusion.16
  155.9 0.0 copy-done
  155.9 0.1 fusion.15
  156.0 0.1 fusion.13
  156.1 0.0 copy-start.1
  156.2 1.6 %fusion.4 = (f32[8,64,128]{2,1,0:T(8,128)}, f32[8,64,128]{2,1,0:T(8,128)}) fusion(f32[12,80,128]{2,1,0:T(8,128)S(1)} %copy-done, f32[8,64,126]{2,1,0:T(8,128)S(1)} %get-tuple-element.14, f32[8,64,2]{2,1,0:T(8,128)S(1)} %get-tuple-element.16, f32[8,64,2]{2,1,0:T(8,128)S(1)} %get-tuple-element.15, f32[8,64,126]{2,1,0:T(8,128)S(1)} %get-tuple-element.13, ...), kind=kLoop, calls=%fused_computation.5 | loop fusion | flops 2228224 | bytes 3932160 | tf_op jit(solution)/shard_map/mul | solution.py:72
  157.8 0.0 copy-done.1
  157.8 1.3 copy.8
Async XLA Ops:
  153.5 2.4 %copy-start = (f32[12,80,128]{2,1,0:T(8,128)S(1)}, f32[12,80,128]{2,1,0:T(8,128)}, u32[]{:S(2)}) copy-start(f32[12,80,128]{2,1,0:T(8,128)} %get-tuple-element.6) | copy-start | bytes 1474564
  156.1 1.6 %copy-start.1 = (f32[2,2,8,128,128]{4,3,2,1,0:T(8,128)S(1)}, f32[2,2,8,128,128]{4,3,2,1,0:T(8,128)}, u32[]{:S(2)}) copy-start(f32[2,2,8,128,128]{4,3,2,1,0:T(8,128)} %get-tuple-element.20) | copy-start | bytes 6291460
